TPU v7x, 32 devices: a whole 2x2x4 slice. The times are simulated.
32 devices in a mesh: rows: 8 (over z, y), cols: 4 (over x, core).
Axes of the slice: x: 2, y: 2, z: 4, core: 2. Of those that a mesh axis runs over, the one named last changes fastest.
Arguments:
- adjacency_tiles: bfloat16 [192, 12, 128, 128], P(('rows', 'cols')), may hold values from 2.170139e-08 to 0.25
- col_block: int32 [192, 12], P(('rows', 'cols')), may hold values from 0 to 191, as said below
- label_prior: float32 [24576, 256], P(('rows', 'cols')), may hold values from 0.05 to 20.1
- seed_label: int32 [24576], P(('rows', 'cols')), may hold values from 0 to 255
- seed_mask: int32 [24576], P(('rows', 'cols')), may hold values 0 or 1
Outputs:
- labels: float32 [24576, 256], P(('rows', 'cols'))
Inputs may be any that keep to these rules, and one draw needn't show every extreme that they name: Row block b is held by device b // 6 of rows+cols, whose rows group is b // (6 * 4). col_block[b, 0] = b. For each device, all its tiles that reference blocks of another rows group reference one and the same block of that group, and each device references every rows group.
All inputs are finite; a program needn't handle non-finite values. No bound on the sum of `seed_mask` on one device may be relied on, other than what follows from the above.
Results may differ from a plain program's by a relative error of at most 0.00041.
Values may be sent and summed in bfloat16 or wider, within the bound.
A program may use at most 64 MiB of HBM per device.

v0:
```python
import jax
import jax.numpy as jnp
from jax import lax
from jax.sharding import PartitionSpec as P

HOPS = 4
ALPHA = 0.85
SEED_BOOST = 8.0


def prepare(label_prior, seed_label, seed_mask):
    classes = label_prior.shape[1]
    one_hot = (seed_label[:, None] == jnp.arange(classes, dtype=jnp.int32)[None, :]).astype(
        jnp.float32
    )
    anchor_raw = label_prior + SEED_BOOST * seed_mask[:, None].astype(jnp.float32) * one_hot
    return anchor_raw * (classes / jnp.sum(anchor_raw, axis=1, keepdims=True))


def ask_blocks(owner_group, within, own_group, n_rows):
    group_ids = jnp.arange(n_rows, dtype=jnp.int32)
    matched = owner_group.reshape(-1)[:, None] == group_ids[None, :]
    wanted = jnp.max(jnp.where(matched, within.reshape(-1)[:, None], 0), axis=0)
    wanted = jnp.where(group_ids == own_group, 0, wanted)
    return lax.all_to_all(
        wanted.reshape(n_rows, 1), "rows", split_axis=0, concat_axis=0, tiled=True
    )


def local(adjacency_tiles, col_block, label_prior, seed_label, seed_mask):
    blocks_dev = adjacency_tiles.shape[0]
    degree = adjacency_tiles.shape[1]
    block_rows = adjacency_tiles.shape[2]
    classes = label_prior.shape[1]
    n_rows = lax.axis_size("rows")
    n_cols = lax.axis_size("cols")
    group_size = n_cols * blocks_dev
    own_group = lax.axis_index("rows")
    owner_group = col_block // group_size
    within = col_block % group_size
    table_index = jnp.where(owner_group == own_group, within, group_size + owner_group).reshape(-1)
    anchor = prepare(label_prior, seed_label, seed_mask)
    labels = anchor
    for hop_index in range(HOPS):
        asked = ask_blocks(owner_group, within, own_group, n_rows)
        sent_blocks = labels.astype(jnp.bfloat16).reshape(blocks_dev, block_rows, classes)
        group_blocks = lax.all_gather(sent_blocks, "cols", axis=0, tiled=True)
        reply = group_blocks[asked[:, 0]]
        remote = lax.all_to_all(reply, "rows", split_axis=0, concat_axis=0, tiled=True)
        table = jnp.concatenate([group_blocks, remote], axis=0)
        operand = table[table_index].reshape(blocks_dev, degree, block_rows, classes)
        spread = jnp.einsum(
            "bkij,bkjc->bic", adjacency_tiles, operand, preferred_element_type=jnp.float32
        )
        spread = spread.reshape(blocks_dev * block_rows, classes)
        blended = ALPHA * spread + (1.0 - ALPHA) * anchor
        labels = blended * (classes / jnp.sum(blended, axis=1, keepdims=True))
    return labels


def solution(mesh):
    in_specs = (
        P(("rows", "cols"), None, None, None),
        P(("rows", "cols"), None),
        P(("rows", "cols"), None),
        P(("rows", "cols")),
        P(("rows", "cols")),
    )
    out_specs = P(("rows", "cols"), None)
    return jax.shard_map(local, mesh=mesh, in_specs=in_specs, out_specs=out_specs, check_vma=False)
```

profile of v0, /device:TPU:0, one launch (start us, length us, event | category | flops | bytes accessed | tf_op | source)
XLA Modules:
  0.0 247.3 jit_solution(12359041004204754055)
XLA Ops:
  6.5 0.0 copy-start
  6.5 0.0 copy-start.3
  6.5 0.0 all-gather.5.cloned.1.call-start
  6.5 0.9 convert_multiply_fusion
  7.4 1.5 fusion.11
  8.9 2.3 multiply_convert_fusion.3
  11.2 0.0 all-gather.5.cloned.1.call-update
  11.2 0.0 copy-done.3
  11.3 0.1 eq.37
  11.3 0.1 broadcast_in_dim.56
  11.4 0.1 select_reduce_fusion
  11.5 0.1 copy.8
  11.6 13.6 %all_to_all.32 = s32[8,1,1]{2,1,0:T(1,128)S(1)} all-to-all(s32[8,1,1]{2,1,0:T(1,128)S(1)} %copy.8), channel_id=1, replica_groups=mesh['rows'=8,'cols'=4] {'rows'}, dimensions={0} | all-to-all | bytes 64 | tf_op jit(solution)/shard_map/all_to_all | solution.py:25
  25.2 0.2 reduce
  25.5 8.3 %all-gather.5.cloned.1.call-done = bf16[24,128,256]{2,1,0:T(8,128)(2,1)} async-done(((bf16[6,128,256]{2,1,0:T(8,128)(2,1)}), bf16[24,128,256]{2,1,0:T(8,128)(2,1)}) %all-gather.5.cloned.1.call-update) | async-done | bytes 1572880 | tf_op jit(solution)/shard_map/all_gather | solution.py:47
  33.7 2.8 %gather_fusion = bf16[8,128,256]{2,1,0:T(8,128)(2,1)} fusion(bf16[24,128,256]{2,1,0:T(8,128)(2,1)} %all-gather.5.cloned.1.call-done, s32[1024]{0:T(1024)S(1)} %pad_clamp_fusion.1), kind=kCustom, calls=%fused_computation | custom fusion | bytes 1048608 | tf_op jit(solution)/shard_map/gather | solution.py:48
  36.5 5.5 %all-to-all-start.1 = ((bf16[8,128,256]{2,1,0:T(8,128)(2,1)}), bf16[8,128,256]{2,1,0:T(8,128)(2,1)S(1)}, u32[]{:S(2)}, u32[]{:S(2)}) async-start(bf16[8,128,256]{2,1,0:T(8,128)(2,1)} %gather_fusion), calls=%async_computation.1 | async-start | bytes 1048576 | tf_op jit(solution)/shard_map/all_to_all | solution.py:49
  42.0 0.0 all-gather.7.cloned.1.call-start
  42.1 0.1 reshape.143
  42.2 14.7 %all-to-all-done.1 = bf16[8,128,256]{2,1,0:T(8,128)(2,1)S(1)} async-done(((bf16[8,128,256]{2,1,0:T(8,128)(2,1)}), bf16[8,128,256]{2,1,0:T(8,128)(2,1)S(1)}, u32[]{:S(2)}, u32[]{:S(2)}) %all-to-all-start.1) | async-done | bytes 524320 | tf_op jit(solution)/shard_map/all_to_all | solution.py:49
  56.9 3.0 %pad_maximum_fusion = bf16[32,128,256]{2,1,0:T(8,128)(2,1)} fusion(bf16[8,128,256]{2,1,0:T(8,128)(2,1)S(1)} %all-to-all-done.1, bf16[24,128,256]{2,1,0:T(8,128)(2,1)} %all-gather.5.cloned.1.call-done), kind=kLoop, calls=%fused_computation.8 | loop fusion | flops 1048576 | bytes 4194304 | tf_op jit(solution)/shard_map/concatenate | solution.py:50
  59.9 7.0 %gather_fusion.1 = bf16[72,128,256]{2,1,0:T(8,128)(2,1)} fusion(bf16[32,128,256]{2,1,0:T(8,128)(2,1)} %pad_maximum_fusion, s32[1024]{0:T(1024)S(1)} %pad_clamp_fusion), kind=kCustom, calls=%fused_computation.1 | custom fusion | bytes 9437472 | tf_op jit(solution)/shard_map/gather | solution.py:51
  66.9 0.0 copy-done
  66.9 0.0 copy-start.1
  66.9 0.0 copy-start.2
  66.9 3.3 %fusion = f32[6,256,128]{1,2,0:T(8,128)S(1)} fusion(bf16[6,12,128,128]{3,2,1,0:T(8,128)(2,1)S(1)} %copy-done, bf16[6,12,128,256]{3,2,1,0:T(8,128)(2,1)} %bitcast.77), kind=kOutput, calls=%fused_computation.16 | convolution fusion | flops 604176384 | bytes 7864320 | tf_op jit(solution)/shard_map/bkij,bkjc->bic/dot_general | solution.py:52
  70.2 0.0 copy-done.1
  70.3 0.0 copy-done.2
  70.3 0.5 fusion.4
  70.8 1.3 multiply_convert_fusion.2
  72.1 0.0 all-gather.7.cloned.1.call-update
  72.1 0.0 all-gather.9.cloned.1.call-start
  72.1 17.9 %all-gather.7.cloned.1.call-done = bf16[24,128,256]{2,1,0:T(8,128)(2,1)} async-done(((bf16[6,128,256]{2,1,0:T(8,128)(2,1)}), bf16[24,128,256]{2,1,0:T(8,128)(2,1)}) %all-gather.7.cloned.1.call-update) | async-done | bytes 1572880 | tf_op jit(solution)/shard_map/all_gather | solution.py:47
  90.0 2.8 %gather_fusion.2 = bf16[8,128,256]{2,1,0:T(8,128)(2,1)} fusion(bf16[24,128,256]{2,1,0:T(8,128)(2,1)} %all-gather.7.cloned.1.call-done, s32[1024]{0:T(1024)S(1)} %pad_clamp_fusion.1), kind=kCustom, calls=%fused_computation.2 | custom fusion | bytes 1048608 | tf_op jit(solution)/shard_map/gather | solution.py:48
  92.8 20.4 %all_to_all.33 = bf16[8,128,256]{2,1,0:T(8,128)(2,1)S(1)} all-to-all(bf16[8,128,256]{2,1,0:T(8,128)(2,1)} %gather_fusion.2), channel_id=1, replica_groups=mesh['rows'=8,'cols'=4] {'rows'}, dimensions={0} | all-to-all | bytes 1048576 | tf_op jit(solution)/shard_map/all_to_all | solution.py:49
  113.2 3.0 %pad_maximum_fusion.1 = bf16[32,128,256]{2,1,0:T(8,128)(2,1)} fusion(bf16[8,128,256]{2,1,0:T(8,128)(2,1)S(1)} %all_to_all.33, bf16[24,128,256]{2,1,0:T(8,128)(2,1)} %all-gather.7.cloned.1.call-done), kind=kLoop, calls=%fused_computation.9 | loop fusion | flops 1048576 | bytes 4194304 | tf_op jit(solution)/shard_map/concatenate | solution.py:50
  116.1 7.0 %gather_fusion.3 = bf16[72,128,256]{2,1,0:T(8,128)(2,1)} fusion(bf16[32,128,256]{2,1,0:T(8,128)(2,1)} %pad_maximum_fusion.1, s32[1024]{0:T(1024)S(1)} %pad_clamp_fusion), kind=kCustom, calls=%fused_computation.3 | custom fusion | bytes 9437472 | tf_op jit(solution)/shard_map/gather | solution.py:51
  123.2 3.2 %fusion.1 = f32[6,256,128]{1,2,0:T(8,128)S(1)} fusion(bf16[6,12,128,128]{3,2,1,0:T(8,128)(2,1)S(1)} %copy-done, bf16[6,12,128,256]{3,2,1,0:T(8,128)(2,1)} %bitcast.78), kind=kOutput, calls=%fused_computation.17 | convolution fusion | flops 604176384 | bytes 7864320 | tf_op jit(solution)/shard_map/bkij,bkjc->bic/dot_general | solution.py:52
  126.4 0.5 fusion.5
  127.0 1.3 multiply_convert_fusion.1
  128.2 0.0 all-gather.9.cloned.1.call-update
  128.3 0.0 all-gather.11.cloned.1.call-start
  128.3 17.9 %all-gather.9.cloned.1.call-done = bf16[24,128,256]{2,1,0:T(8,128)(2,1)} async-done(((bf16[6,128,256]{2,1,0:T(8,128)(2,1)}), bf16[24,128,256]{2,1,0:T(8,128)(2,1)}) %all-gather.9.cloned.1.call-update) | async-done | bytes 1572880 | tf_op jit(solution)/shard_map/all_gather | solution.py:47
  146.2 2.8 %gather_fusion.4 = bf16[8,128,256]{2,1,0:T(8,128)(2,1)} fusion(bf16[24,128,256]{2,1,0:T(8,128)(2,1)} %all-gather.9.cloned.1.call-done, s32[1024]{0:T(1024)S(1)} %pad_clamp_fusion.1), kind=kCustom, calls=%fused_computation.4 | custom fusion | bytes 1048608 | tf_op jit(solution)/shard_map/gather | solution.py:48
  149.0 20.4 %all_to_all.34 = bf16[8,128,256]{2,1,0:T(8,128)(2,1)S(1)} all-to-all(bf16[8,128,256]{2,1,0:T(8,128)(2,1)} %gather_fusion.4), channel_id=1, replica_groups=mesh['rows'=8,'cols'=4] {'rows'}, dimensions={0} | all-to-all | bytes 1048576 | tf_op jit(solution)/shard_map/all_to_all | solution.py:49
  169.4 3.0 %pad_maximum_fusion.2 = bf16[32,128,256]{2,1,0:T(8,128)(2,1)} fusion(bf16[8,128,256]{2,1,0:T(8,128)(2,1)S(1)} %all_to_all.34, bf16[24,128,256]{2,1,0:T(8,128)(2,1)} %all-gather.9.cloned.1.call-done), kind=kLoop, calls=%fused_computation.10 | loop fusion | flops 1048576 | bytes 4194304 | tf_op jit(solution)/shard_map/concatenate | solution.py:50
  172.3 7.0 %gather_fusion.5 = bf16[72,128,256]{2,1,0:T(8,128)(2,1)} fusion(bf16[32,128,256]{2,1,0:T(8,128)(2,1)} %pad_maximum_fusion.2, s32[1024]{0:T(1024)S(1)} %pad_clamp_fusion), kind=kCustom, calls=%fused_computation.5 | custom fusion | bytes 9437472 | tf_op jit(solution)/shard_map/gather | solution.py:51
  179.4 3.2 %fusion.2 = f32[6,256,128]{1,2,0:T(8,128)S(1)} fusion(bf16[6,12,128,128]{3,2,1,0:T(8,128)(2,1)S(1)} %copy-done, bf16[6,12,128,256]{3,2,1,0:T(8,128)(2,1)} %bitcast.79), kind=kOutput, calls=%fused_computation.18 | convolution fusion | flops 604176384 | bytes 7864320 | tf_op jit(solution)/shard_map/bkij,bkjc->bic/dot_general | solution.py:52
  182.6 0.5 fusion.6
  183.2 1.3 multiply_convert_fusion
  184.4 0.0 all-gather.11.cloned.1.call-update
  184.5 17.9 %all-gather.11.cloned.1.call-done = bf16[24,128,256]{2,1,0:T(8,128)(2,1)} async-done(((bf16[6,128,256]{2,1,0:T(8,128)(2,1)}), bf16[24,128,256]{2,1,0:T(8,128)(2,1)}) %all-gather.11.cloned.1.call-update) | async-done | bytes 1572880 | tf_op jit(solution)/shard_map/all_gather | solution.py:47
  202.4 2.8 %gather_fusion.6 = bf16[8,128,256]{2,1,0:T(8,128)(2,1)} fusion(bf16[24,128,256]{2,1,0:T(8,128)(2,1)} %all-gather.11.cloned.1.call-done, s32[1024]{0:T(1024)S(1)} %pad_clamp_fusion.1), kind=kCustom, calls=%fused_computation.6 | custom fusion | bytes 1048608 | tf_op jit(solution)/shard_map/gather | solution.py:48
  205.2 20.4 %all_to_all.35 = bf16[8,128,256]{2,1,0:T(8,128)(2,1)S(1)} all-to-all(bf16[8,128,256]{2,1,0:T(8,128)(2,1)} %gather_fusion.6), channel_id=1, replica_groups=mesh['rows'=8,'cols'=4] {'rows'}, dimensions={0} | all-to-all | bytes 1048576 | tf_op jit(solution)/shard_map/all_to_all | solution.py:49
  225.6 3.0 %pad_maximum_fusion.3 = bf16[32,128,256]{2,1,0:T(8,128)(2,1)} fusion(bf16[8,128,256]{2,1,0:T(8,128)(2,1)S(1)} %all_to_all.35, bf16[24,128,256]{2,1,0:T(8,128)(2,1)} %all-gather.11.cloned.1.call-done), kind=kLoop, calls=%fused_computation.11 | loop fusion | flops 1048576 | bytes 4194304 | tf_op jit(solution)/shard_map/concatenate | solution.py:50
  228.5 7.0 %gather_fusion.7 = bf16[72,128,256]{2,1,0:T(8,128)(2,1)} fusion(bf16[32,128,256]{2,1,0:T(8,128)(2,1)} %pad_maximum_fusion.3, s32[1024]{0:T(1024)S(1)} %pad_clamp_fusion), kind=kCustom, calls=%fused_computation.7 | custom fusion | bytes 9437472 | tf_op jit(solution)/shard_map/gather | solution.py:51
  235.6 3.2 %fusion.3 = f32[6,256,128]{1,2,0:T(8,128)S(1)} fusion(bf16[6,12,128,128]{3,2,1,0:T(8,128)(2,1)S(1)} %copy-done, bf16[6,12,128,256]{3,2,1,0:T(8,128)(2,1)} %bitcast.76), kind=kOutput, calls=%fused_computation.19 | convolution fusion | flops 604176384 | bytes 7864320 | tf_op jit(solution)/shard_map/bkij,bkjc->bic/dot_general | solution.py:52
  238.8 0.5 fusion.7
  239.3 1.4 broadcast_multiply_fusion
  (11 shorter events, 0.1 us)
Async XLA Ops:
  6.5 60.4 %copy-start = (bf16[6,12,128,128]{3,2,1,0:T(8,128)(2,1)S(1)}, bf16[6,12,128,128]{3,2,1,0:T(8,128)(2,1)}, u32[]{:S(2)}) copy-start(bf16[6,12,128,128]{3,2,1,0:T(8,128)(2,1)} %param.5) | copy-start | bytes 7077892
  6.5 4.7 %copy-start.3 = (s32[6,12]{1,0:T(8,128)S(1)}, s32[6,12]{1,0:T(8,128)}, u32[]{:S(2)}) copy-start(s32[6,12]{1,0:T(8,128)} %param.6) | copy-start | bytes 868
  6.5 27.2 %all-gather.5.cloned.1.call-start = ((), (), s32[]{:S(2)}) async-start(), calls=%async_computation.5 | async-start | bytes 1966080 | tf_op jit(solution)/shard_map/all_gather | solution.py:47
  36.5 20.4 %all-to-all-start.1 = ((bf16[8,128,256]{2,1,0:T(8,128)(2,1)}), bf16[8,128,256]{2,1,0:T(8,128)(2,1)S(1)}, u32[]{:S(2)}, u32[]{:S(2)}) async-start(bf16[8,128,256]{2,1,0:T(8,128)(2,1)} %gather_fusion), calls=%async_computation.1 | async-start | bytes 1048576 | tf_op jit(solution)/shard_map/all_to_all | solution.py:49
  42.0 48.0 %all-gather.7.cloned.1.call-start = ((), (), s32[]{:S(2)}) async-start(), calls=%async_computation.6 | async-start | bytes 1966080 | tf_op jit(solution)/shard_map/all_gather | solution.py:47
  66.9 3.3 %copy-start.1 = (f32[768,256]{1,0:T(8,128)S(1)}, f32[768,256]{1,0:T(8,128)}, u32[]{:S(2)}) copy-start(f32[768,256]{1,0:T(8,128)} %param.7) | copy-start | bytes 2359300
  66.9 3.3 %copy-start.2 = (s32[768]{0:T(1024)S(1)}, s32[768]{0:T(1024)}, u32[]{:S(2)}) copy-start(s32[768]{0:T(1024)} %param.8) | copy-start | bytes 9220
  72.1 74.1 %all-gather.9.cloned.1.call-start = ((), (), s32[]{:S(2)}) async-start(), calls=%async_computation.7 | async-start | bytes 1966080 | tf_op jit(solution)/shard_map/all_gather | solution.py:47
  128.3 74.1 %all-gather.11.cloned.1.call-start = ((), (), s32[]{:S(2)}) async-start(), calls=%async_computation.8 | async-start | bytes 1966080 | tf_op jit(solution)/shard_map/all_gather | solution.py:47
Sparse Core Ops, SparseCore 0:
  11.3 22.3 all-gather.4
  72.2 17.7 all-gather.6
  128.4 17.7 all-gather.8
  184.6 17.7 all-gather.10
where the time goes:
time: 248 us; the launch traced here: 247 us
  waiting for transfers between devices  76.7 us (31%)
  blocking collectives  74.8 us (30%)
  local copies, waits for them, and re-layouts  39.6 us (16%)
  other arithmetic  24.2 us (10%)
  between operations  13.3 us (5%)
  matrix products  13 us (5%)
  starting transfers between devices  5.64 us (2%)
    all_gather x4, waiting for transfers between devices, local(): group_blocks = lax.all_gather(sent_blocks, 'cols', axis=0, tiled=True)  61.9 us
    all_to_all x3, blocking collectives, local(): lax.all_to_all(reply, 'rows', split_axis=0, concat_axis=0, tiled=True)  61.2 us
    gather x4, local copies, waits for them, and re-layouts, local(): table[table_index].reshape(blocks_dev, degree, block_rows, classes)  28.2 us
    all_to_all x1, waiting for transfers between devices, local(): lax.all_to_all(reply, 'rows', split_axis=0, concat_axis=0, tiled=True)  14.7 us
    all_to_all x1, blocking collectives, ask_blocks(): lax.all_to_all(wanted.reshape(n_rows, 1), 'rows', split_axis=0, concat_ax...  13.6 us
    dot_general x4, matrix products, local(): jnp.einsum('bkij,bkjc->bic', adjacency_tiles, operand, preferred_element_...  13 us
    concatenate x4, other arithmetic, local(): table = jnp.concatenate([group_blocks, remote], axis=0)  11.8 us
    gather x4, local copies, waits for them, and re-layouts, local(): reply = group_blocks[asked[:, 0]]  11.1 us
  transfers between devices with their start and end apart: 5, of which 5 were waited for; matrix products, arithmetic and copies ran while one was open for 0% of the time, Pallas kernels for 0%

commit v1 on v0

--- a/solution.py
+++ b/solution.py
@@ -46,7 +46,18 @@
         sent_blocks = labels.astype(jnp.bfloat16).reshape(blocks_dev, block_rows, classes)
         group_blocks = lax.all_gather(sent_blocks, "cols", axis=0, tiled=True)
         reply = group_blocks[asked[:, 0]]
-        remote = lax.all_to_all(reply, "rows", split_axis=0, concat_axis=0, tiled=True)
+        ways, here = (lax.axis_size("rows"), lax.axis_index("rows"))
+        width = reply.shape[0] // ways
+        dims = list(reply.shape)
+        dims[0] = width
+        height = dims[0]
+        dims[0] = height * ways
+        remote = jnp.zeros(dims, reply.dtype)
+        for mask in range(ways):
+            part = lax.dynamic_slice_in_dim(reply, (here ^ mask) * width, width, axis=0)
+            if mask:
+                part = lax.ppermute(part, "rows", [(d, d ^ mask) for d in range(ways)])
+            remote = lax.dynamic_update_slice_in_dim(remote, part, (here ^ mask) * height, axis=0)
         table = jnp.concatenate([group_blocks, remote], axis=0)
         operand = table[table_index].reshape(blocks_dev, degree, block_rows, classes)
         spread = jnp.einsum(

time: 248 us -> 238 us (0.960)
  blocking collectives: 74.8 us -> 0 us
  starting transfers between devices: 5.64 us -> 52.7 us
  waiting for transfers between devices: 76.7 us -> 95.5 us
  other arithmetic: 24.2 us -> 18.5 us
  local copies, waits for them, and re-layouts: 39.6 us -> 43.6 us
    all_to_all x4 -> x0, blocking collectives: 74.8 us -> none  [the longest x3 61.2 us: local(): lax.all_to_all(reply, 'rows', split_axis=0, concat_axis=0, tiled=True)]
    ppermute x0 -> x28, starting transfers between devices: none -> 45.1 us  [local(): part = lax.ppermute(part, 'rows', [(d, d ^ mask) for d in range(ways)])]
    ppermute x0 -> x28, waiting for transfers between devices: none -> 25.9 us  [local(): part = lax.ppermute(part, 'rows', [(d, d ^ mask) for d in range(ways)])]
    all_to_all x1, waiting for transfers between devices: 14.7 us -> 6.33 us  [ask_blocks(): lax.all_to_all(wanted.reshape(n_rows, 1), 'rows', split_axis=0, concat_ax...]
    concatenate x4, other arithmetic: 11.8 us -> 6.18 us  [local(): table = jnp.concatenate([group_blocks, remote], axis=0)]
    dynamic_slice x0 -> x4, local copies, waits for them, and re-layouts: none -> 3.72 us  [local(): part = lax.dynamic_slice_in_dim(reply, (here ^ mask) * width, width, axis=0)]
  transfers between devices with their start and end apart: 5 -> 33, of which waited for: 5 -> 13; matrix products, arithmetic and copies ran while one was open for 0% -> 1% of each run, Pallas kernels for 0% -> 0%
where the time goes in v1:
time: 238 us; the launch traced here: 237 us
  waiting for transfers between devices  95.5 us (40%)
  starting transfers between devices  52.7 us (22%)
  local copies, waits for them, and re-layouts  43.6 us (18%)
  other arithmetic  18.5 us (8%)
  between operations  13.7 us (6%)
  matrix products  13.1 us (6%)
    all_gather x4, waiting for transfers between devices, local(): group_blocks = lax.all_gather(sent_blocks, 'cols', axis=0, tiled=True)  63.2 us
    ppermute x28, starting transfers between devices, local(): part = lax.ppermute(part, 'rows', [(d, d ^ mask) for d in range(ways)])  45.1 us
    gather x4, local copies, waits for them, and re-layouts, local(): table[table_index].reshape(blocks_dev, degree, block_rows, classes)  28.3 us
    ppermute x28, waiting for transfers between devices, local(): part = lax.ppermute(part, 'rows', [(d, d ^ mask) for d in range(ways)])  25.9 us
    dot_general x4, matrix products, local(): jnp.einsum('bkij,bkjc->bic', adjacency_tiles, operand, preferred_element_...  13.1 us
    gather x4, local copies, waits for them, and re-layouts, local(): reply = group_blocks[asked[:, 0]]  10.3 us
    all_to_all x1, starting transfers between devices, ask_blocks(): lax.all_to_all(wanted.reshape(n_rows, 1), 'rows', split_axis=0, concat_ax...  7.31 us
    all_to_all x1, waiting for transfers between devices, ask_blocks(): lax.all_to_all(wanted.reshape(n_rows, 1), 'rows', split_axis=0, concat_ax...  6.33 us
  transfers between devices with their start and end apart: 33, of which 13 were waited for; matrix products, arithmetic and copies ran while one was open for 1% of the time, Pallas kernels for 0%

profile of v1, /device:TPU:0, one launch (start us, length us, event | category | flops | bytes accessed | tf_op | source)
XLA Modules:
  0.0 237.0 jit_solution(4067101596776896205)
XLA Ops:
  6.5 0.9 convert_multiply_fusion
  7.4 1.5 fusion.11
  8.9 2.3 multiply_convert_fusion.3
  11.5 0.7 copy.8
  12.2 7.3 %all-to-all-start = ((s32[8,1,1]{2,1,0:T(1,128)}), s32[8,1,1]{2,1,0:T(1,128)S(1)}, u32[]{:S(2)}, u32[]{:S(2)}) async-start(s32[8,1,1]{2,1,0:T(1,128)} %copy.8), calls=%async_computation | async-start | bytes 8192 | tf_op jit(solution)/shard_map/all_to_all | solution.py:25
  19.7 6.3 %all-to-all-done = s32[8,1,1]{2,1,0:T(1,128)S(1)} async-done(((s32[8,1,1]{2,1,0:T(1,128)}), s32[8,1,1]{2,1,0:T(1,128)S(1)}, u32[]{:S(2)}, u32[]{:S(2)}) %all-to-all-start) | async-done | bytes 64 | tf_op jit(solution)/shard_map/all_to_all | solution.py:25
  26.3 7.5 %all-gather.5.cloned.1.call-done = bf16[24,128,256]{2,1,0:T(8,128)(2,1)} async-done(((bf16[6,128,256]{2,1,0:T(8,128)(2,1)}), bf16[24,128,256]{2,1,0:T(8,128)(2,1)}) %all-gather.5.cloned.1.call-update) | async-done | bytes 1572880 | tf_op jit(solution)/shard_map/all_gather | solution.py:47
  33.7 2.0 gather_fusion
  35.8 1.6 collective-permute-start
  37.4 1.5 collective-permute-start.1
  39.4 2.4 %collective-permute-start.3 = (bf16[1,128,256]{2,1,0:T(8,128)(2,1)S(1)}, bf16[1,128,256]{2,1,0:T(8,128)(2,1)S(1)}, u32[]{:S(2)}, u32[]{:S(2)}) collective-permute-start(bf16[1,128,256]{2,1,0:T(8,128)(2,1)S(1)} %get-tuple-element.32), channel_id=1, source_target_pairs={{0,16},{4,20},{8,24},{12,28},{16,0},{20,4},{24,8},{28,12},{1,17},{... | collective-permute-start | bytes 196616 | tf_op jit(solution)/shard_map/ppermute | solution.py:59
  41.8 1.5 collective-permute-start.4
  43.3 3.3 %collective-permute-start.5 = (bf16[1,128,256]{2,1,0:T(8,128)(2,1)S(1)}, bf16[1,128,256]{2,1,0:T(8,128)(2,1)S(1)}, u32[]{:S(2)}, u32[]{:S(2)}) collective-permute-start(bf16[1,128,256]{2,1,0:T(8,128)(2,1)S(1)} %get-tuple-element.30), channel_id=1, source_target_pairs={{0,24},{4,28},{8,16},{12,20},{16,8},{20,12},{24,0},{28,4},{1,25},{... | collective-permute-start | bytes 196616 | tf_op jit(solution)/shard_map/ppermute | solution.py:59
  47.2 5.0 %collective-permute-done.4 = bf16[1,128,256]{2,1,0:T(8,128)(2,1)S(1)} collective-permute-done((bf16[1,128,256]{2,1,0:T(8,128)(2,1)S(1)}, bf16[1,128,256]{2,1,0:T(8,128)(2,1)S(1)}, u32[]{:S(2)}, u32[]{:S(2)}) %collective-permute-start.4) | collective-permute-done | bytes 65568 | tf_op jit(solution)/shard_map/ppermute | solution.py:59
  52.3 1.4 collective-permute-done.6
  53.7 1.5 pad_maximum_fusion
  55.3 7.1 %gather_fusion.1 = bf16[72,128,256]{2,1,0:T(8,128)(2,1)} fusion(bf16[32,128,256]{2,1,0:T(8,128)(2,1)} %pad_maximum_fusion, s32[1024]{0:T(1024)S(1)} %pad_clamp_fusion), kind=kCustom, calls=%fused_computation.1 | custom fusion | bytes 9437472 | tf_op jit(solution)/shard_map/gather | solution.py:62
  62.4 3.3 %fusion = f32[6,256,128]{1,2,0:T(8,128)S(1)} fusion(bf16[6,12,128,128]{3,2,1,0:T(8,128)(2,1)S(1)} %copy-done, bf16[6,12,128,256]{3,2,1,0:T(8,128)(2,1)} %bitcast.77), kind=kOutput, calls=%fused_computation.16 | convolution fusion | flops 604176384 | bytes 7864320 | tf_op jit(solution)/shard_map/bkij,bkjc->bic/dot_general | solution.py:63
  66.2 1.3 multiply_convert_fusion.2
  67.6 18.6 %all-gather.7.cloned.1.call-done = bf16[24,128,256]{2,1,0:T(8,128)(2,1)} async-done(((bf16[6,128,256]{2,1,0:T(8,128)(2,1)}), bf16[24,128,256]{2,1,0:T(8,128)(2,1)}) %all-gather.7.cloned.1.call-update) | async-done | bytes 1572880 | tf_op jit(solution)/shard_map/all_gather | solution.py:47
  86.2 2.8 %gather_fusion.2 = bf16[8,128,256]{2,1,0:T(8,128)(2,1)} fusion(bf16[24,128,256]{2,1,0:T(8,128)(2,1)} %all-gather.7.cloned.1.call-done, s32[1024]{0:T(1024)S(1)} %pad_clamp_fusion.1), kind=kCustom, calls=%fused_computation.2 | custom fusion | bytes 1048608 | tf_op jit(solution)/shard_map/gather | solution.py:48
  89.0 1.2 constant_dynamic-slice_fusion.13
  90.2 1.5 collective-permute-start.7
  91.8 1.5 collective-permute-start.8
  93.8 2.4 %collective-permute-start.10 = (bf16[1,128,256]{2,1,0:T(8,128)(2,1)S(1)}, bf16[1,128,256]{2,1,0:T(8,128)(2,1)S(1)}, u32[]{:S(2)}, u32[]{:S(2)}) collective-permute-start(bf16[1,128,256]{2,1,0:T(8,128)(2,1)S(1)} %get-tuple-element.24), channel_id=1, source_target_pairs={{0,16},{4,20},{8,24},{12,28},{16,0},{20,4},{24,8},{28,12},{1,17},{... | collective-permute-start | bytes 196616 | tf_op jit(solution)/shard_map/ppermute | solution.py:59
  96.2 1.4 collective-permute-start.11
  97.6 3.3 %collective-permute-start.12 = (bf16[1,128,256]{2,1,0:T(8,128)(2,1)S(1)}, bf16[1,128,256]{2,1,0:T(8,128)(2,1)S(1)}, u32[]{:S(2)}, u32[]{:S(2)}) collective-permute-start(bf16[1,128,256]{2,1,0:T(8,128)(2,1)S(1)} %get-tuple-element.22), channel_id=1, source_target_pairs={{0,24},{4,28},{8,16},{12,20},{16,8},{20,12},{24,0},{28,4},{1,25},{... | collective-permute-start | bytes 196616 | tf_op jit(solution)/shard_map/ppermute | solution.py:59
  101.0 0.5 collective-permute-start.13
  101.6 5.0 %collective-permute-done.11 = bf16[1,128,256]{2,1,0:T(8,128)(2,1)S(1)} collective-permute-done((bf16[1,128,256]{2,1,0:T(8,128)(2,1)S(1)}, bf16[1,128,256]{2,1,0:T(8,128)(2,1)S(1)}, u32[]{:S(2)}, u32[]{:S(2)}) %collective-permute-start.11) | collective-permute-done | bytes 65568 | tf_op jit(solution)/shard_map/ppermute | solution.py:59
  106.7 1.4 collective-permute-done.13
  108.1 1.5 pad_maximum_fusion.1
  109.7 7.1 %gather_fusion.3 = bf16[72,128,256]{2,1,0:T(8,128)(2,1)} fusion(bf16[32,128,256]{2,1,0:T(8,128)(2,1)} %pad_maximum_fusion.1, s32[1024]{0:T(1024)S(1)} %pad_clamp_fusion), kind=kCustom, calls=%fused_computation.3 | custom fusion | bytes 9437472 | tf_op jit(solution)/shard_map/gather | solution.py:62
  116.7 3.2 %fusion.1 = f32[6,256,128]{1,2,0:T(8,128)S(1)} fusion(bf16[6,12,128,128]{3,2,1,0:T(8,128)(2,1)S(1)} %copy-done, bf16[6,12,128,256]{3,2,1,0:T(8,128)(2,1)} %bitcast.78), kind=kOutput, calls=%fused_computation.17 | convolution fusion | flops 604176384 | bytes 7864320 | tf_op jit(solution)/shard_map/bkij,bkjc->bic/dot_general | solution.py:63
  120.5 1.3 multiply_convert_fusion.1
  122.1 18.4 %all-gather.9.cloned.1.call-done = bf16[24,128,256]{2,1,0:T(8,128)(2,1)} async-done(((bf16[6,128,256]{2,1,0:T(8,128)(2,1)}), bf16[24,128,256]{2,1,0:T(8,128)(2,1)}) %all-gather.9.cloned.1.call-update) | async-done | bytes 1572880 | tf_op jit(solution)/shard_map/all_gather | solution.py:47
  140.5 2.8 %gather_fusion.4 = bf16[8,128,256]{2,1,0:T(8,128)(2,1)} fusion(bf16[24,128,256]{2,1,0:T(8,128)(2,1)} %all-gather.9.cloned.1.call-done, s32[1024]{0:T(1024)S(1)} %pad_clamp_fusion.1), kind=kCustom, calls=%fused_computation.4 | custom fusion | bytes 1048608 | tf_op jit(solution)/shard_map/gather | solution.py:48
  143.3 1.2 constant_dynamic-slice_fusion.6
  144.5 1.5 collective-permute-start.14
  146.1 1.5 collective-permute-start.15
  148.1 2.4 %collective-permute-start.17 = (bf16[1,128,256]{2,1,0:T(8,128)(2,1)S(1)}, bf16[1,128,256]{2,1,0:T(8,128)(2,1)S(1)}, u32[]{:S(2)}, u32[]{:S(2)}) collective-permute-start(bf16[1,128,256]{2,1,0:T(8,128)(2,1)S(1)} %get-tuple-element.16), channel_id=1, source_target_pairs={{0,16},{4,20},{8,24},{12,28},{16,0},{20,4},{24,8},{28,12},{1,17},{... | collective-permute-start | bytes 196616 | tf_op jit(solution)/shard_map/ppermute | solution.py:59
  150.5 1.4 collective-permute-start.18
  151.9 3.3 %collective-permute-start.19 = (bf16[1,128,256]{2,1,0:T(8,128)(2,1)S(1)}, bf16[1,128,256]{2,1,0:T(8,128)(2,1)S(1)}, u32[]{:S(2)}, u32[]{:S(2)}) collective-permute-start(bf16[1,128,256]{2,1,0:T(8,128)(2,1)S(1)} %get-tuple-element.14), channel_id=1, source_target_pairs={{0,24},{4,28},{8,16},{12,20},{16,8},{20,12},{24,0},{28,4},{1,25},{... | collective-permute-start | bytes 196616 | tf_op jit(solution)/shard_map/ppermute | solution.py:59
  155.3 0.5 collective-permute-start.20
  155.9 5.0 %collective-permute-done.18 = bf16[1,128,256]{2,1,0:T(8,128)(2,1)S(1)} collective-permute-done((bf16[1,128,256]{2,1,0:T(8,128)(2,1)S(1)}, bf16[1,128,256]{2,1,0:T(8,128)(2,1)S(1)}, u32[]{:S(2)}, u32[]{:S(2)}) %collective-permute-start.18) | collective-permute-done | bytes 65568 | tf_op jit(solution)/shard_map/ppermute | solution.py:59
  161.0 1.4 collective-permute-done.20
  162.4 1.5 pad_maximum_fusion.2
  164.0 7.1 %gather_fusion.5 = bf16[72,128,256]{2,1,0:T(8,128)(2,1)} fusion(bf16[32,128,256]{2,1,0:T(8,128)(2,1)} %pad_maximum_fusion.2, s32[1024]{0:T(1024)S(1)} %pad_clamp_fusion), kind=kCustom, calls=%fused_computation.5 | custom fusion | bytes 9437472 | tf_op jit(solution)/shard_map/gather | solution.py:62
  171.0 3.2 %fusion.2 = f32[6,256,128]{1,2,0:T(8,128)S(1)} fusion(bf16[6,12,128,128]{3,2,1,0:T(8,128)(2,1)S(1)} %copy-done, bf16[6,12,128,256]{3,2,1,0:T(8,128)(2,1)} %bitcast.79), kind=kOutput, calls=%fused_computation.18 | convolution fusion | flops 604176384 | bytes 7864320 | tf_op jit(solution)/shard_map/bkij,bkjc->bic/dot_general | solution.py:63
  174.8 1.3 multiply_convert_fusion
  176.1 18.7 %all-gather.11.cloned.1.call-done = bf16[24,128,256]{2,1,0:T(8,128)(2,1)} async-done(((bf16[6,128,256]{2,1,0:T(8,128)(2,1)}), bf16[24,128,256]{2,1,0:T(8,128)(2,1)}) %all-gather.11.cloned.1.call-update) | async-done | bytes 1572880 | tf_op jit(solution)/shard_map/all_gather | solution.py:47
  194.8 2.8 %gather_fusion.6 = bf16[8,128,256]{2,1,0:T(8,128)(2,1)} fusion(bf16[24,128,256]{2,1,0:T(8,128)(2,1)} %all-gather.11.cloned.1.call-done, s32[1024]{0:T(1024)S(1)} %pad_clamp_fusion.1), kind=kCustom, calls=%fused_computation.6 | custom fusion | bytes 1048608 | tf_op jit(solution)/shard_map/gather | solution.py:48
  197.6 1.2 constant_dynamic-slice_fusion.20
  198.8 1.5 collective-permute-start.21
  200.4 1.5 collective-permute-start.22
  202.4 2.4 %collective-permute-start.24 = (bf16[1,128,256]{2,1,0:T(8,128)(2,1)S(1)}, bf16[1,128,256]{2,1,0:T(8,128)(2,1)S(1)}, u32[]{:S(2)}, u32[]{:S(2)}) collective-permute-start(bf16[1,128,256]{2,1,0:T(8,128)(2,1)S(1)} %get-tuple-element.8), channel_id=1, source_target_pairs={{0,16},{4,20},{8,24},{12,28},{16,0},{20,4},{24,8},{28,12},{1,17},{... | collective-permute-start | bytes 196616 | tf_op jit(solution)/shard_map/ppermute | solution.py:59
  204.8 1.4 collective-permute-start.25
  206.2 3.3 %collective-permute-start.26 = (bf16[1,128,256]{2,1,0:T(8,128)(2,1)S(1)}, bf16[1,128,256]{2,1,0:T(8,128)(2,1)S(1)}, u32[]{:S(2)}, u32[]{:S(2)}) collective-permute-start(bf16[1,128,256]{2,1,0:T(8,128)(2,1)S(1)} %get-tuple-element.6), channel_id=1, source_target_pairs={{0,24},{4,28},{8,16},{12,20},{16,8},{20,12},{24,0},{28,4},{1,25},{... | collective-permute-start | bytes 196616 | tf_op jit(solution)/shard_map/ppermute | solution.py:59
  209.6 0.5 collective-permute-start.27
  210.2 5.0 %collective-permute-done.25 = bf16[1,128,256]{2,1,0:T(8,128)(2,1)S(1)} collective-permute-done((bf16[1,128,256]{2,1,0:T(8,128)(2,1)S(1)}, bf16[1,128,256]{2,1,0:T(8,128)(2,1)S(1)}, u32[]{:S(2)}, u32[]{:S(2)}) %collective-permute-start.25) | collective-permute-done | bytes 65568 | tf_op jit(solution)/shard_map/ppermute | solution.py:59
  215.2 1.4 collective-permute-done.27
  216.7 1.5 pad_maximum_fusion.3
  218.3 7.1 %gather_fusion.7 = bf16[72,128,256]{2,1,0:T(8,128)(2,1)} fusion(bf16[32,128,256]{2,1,0:T(8,128)(2,1)} %pad_maximum_fusion.3, s32[1024]{0:T(1024)S(1)} %pad_clamp_fusion), kind=kCustom, calls=%fused_computation.7 | custom fusion | bytes 9437472 | tf_op jit(solution)/shard_map/gather | solution.py:62
  225.3 3.2 %fusion.3 = f32[6,256,128]{1,2,0:T(8,128)S(1)} fusion(bf16[6,12,128,128]{3,2,1,0:T(8,128)(2,1)S(1)} %copy-done, bf16[6,12,128,256]{3,2,1,0:T(8,128)(2,1)} %bitcast.76), kind=kOutput, calls=%fused_computation.19 | convolution fusion | flops 604176384 | bytes 7864320 | tf_op jit(solution)/shard_map/bkij,bkjc->bic/dot_general | solution.py:63
  229.1 1.4 broadcast_multiply_fusion
  (102 shorter events, 6.3 us)
Async XLA Ops:
  6.5 55.8 %copy-start = (bf16[6,12,128,128]{3,2,1,0:T(8,128)(2,1)S(1)}, bf16[6,12,128,128]{3,2,1,0:T(8,128)(2,1)}, u32[]{:S(2)}) copy-start(bf16[6,12,128,128]{3,2,1,0:T(8,128)(2,1)} %param.5) | copy-start | bytes 7077892
  6.5 4.7 %copy-start.7 = (s32[6,12]{1,0:T(8,128)S(1)}, s32[6,12]{1,0:T(8,128)}, u32[]{:S(2)}) copy-start(s32[6,12]{1,0:T(8,128)} %param.6) | copy-start | bytes 868
  6.5 27.2 %all-gather.5.cloned.1.call-start = ((), (), s32[]{:S(2)}) async-start(), calls=%async_computation.1 | async-start | bytes 1966080 | tf_op jit(solution)/shard_map/all_gather | solution.py:47
  12.2 13.8 %all-to-all-start = ((s32[8,1,1]{2,1,0:T(1,128)}), s32[8,1,1]{2,1,0:T(1,128)S(1)}, u32[]{:S(2)}, u32[]{:S(2)}) async-start(s32[8,1,1]{2,1,0:T(1,128)} %copy.8), calls=%async_computation | async-start | bytes 8192 | tf_op jit(solution)/shard_map/all_to_all | solution.py:25
  19.5 66.7 %all-gather.7.cloned.1.call-start = ((), (), s32[]{:S(2)}) async-start(), calls=%async_computation.2 | async-start | bytes 1966080 | tf_op jit(solution)/shard_map/all_gather | solution.py:47
  35.7 18.0 %copy-start.2 = (bf16[24,128,256]{2,1,0:T(8,128)(2,1)S(1)}, bf16[24,128,256]{2,1,0:T(8,128)(2,1)}, u32[]{:S(2)}) copy-start(bf16[24,128,256]{2,1,0:T(8,128)(2,1)} %all-gather.5.cloned.1.call-done) | copy-start | bytes 4718596
  35.8 7.4 %collective-permute-start = (bf16[1,128,256]{2,1,0:T(8,128)(2,1)S(1)}, bf16[1,128,256]{2,1,0:T(8,128)(2,1)S(1)}, u32[]{:S(2)}, u32[]{:S(2)}) collective-permute-start(bf16[1,128,256]{2,1,0:T(8,128)(2,1)S(1)} %get-tuple-element.35), channel_id=1, source_target_pairs={{0,4},{4,0},{8,12},{12,8},{16,20},{20,16},{24,28},{28,24},{1,5},{5... | collective-permute-start | bytes 196616 | tf_op jit(solution)/shard_map/ppermute | solution.py:59
  37.4 9.2 %collective-permute-start.1 = (bf16[1,128,256]{2,1,0:T(8,128)(2,1)S(1)}, bf16[1,128,256]{2,1,0:T(8,128)(2,1)S(1)}, u32[]{:S(2)}, u32[]{:S(2)}) collective-permute-start(bf16[1,128,256]{2,1,0:T(8,128)(2,1)S(1)} %get-tuple-element.34), channel_id=1, source_target_pairs={{0,8},{4,12},{8,0},{12,4},{16,24},{20,28},{24,16},{28,20},{1,9},{5... | collective-permute-start | bytes 196616 | tf_op jit(solution)/shard_map/ppermute | solution.py:59
  38.9 8.3 %collective-permute-start.2 = (bf16[1,128,256]{2,1,0:T(8,128)(2,1)S(1)}, bf16[1,128,256]{2,1,0:T(8,128)(2,1)S(1)}, u32[]{:S(2)}, u32[]{:S(2)}) collective-permute-start(bf16[1,128,256]{2,1,0:T(8,128)(2,1)S(1)} %get-tuple-element.33), channel_id=1, source_target_pairs={{0,12},{4,8},{8,4},{12,0},{16,28},{20,24},{24,20},{28,16},{1,13},{... | collective-permute-start | bytes 196616 | tf_op jit(solution)/shard_map/ppermute | solution.py:59
  39.4 7.8 %collective-permute-start.3 = (bf16[1,128,256]{2,1,0:T(8,128)(2,1)S(1)}, bf16[1,128,256]{2,1,0:T(8,128)(2,1)S(1)}, u32[]{:S(2)}, u32[]{:S(2)}) collective-permute-start(bf16[1,128,256]{2,1,0:T(8,128)(2,1)S(1)} %get-tuple-element.32), channel_id=1, source_target_pairs={{0,16},{4,20},{8,24},{12,28},{16,0},{20,4},{24,8},{28,12},{1,17},{... | collective-permute-start | bytes 196616 | tf_op jit(solution)/shard_map/ppermute | solution.py:59
  41.8 10.4 %collective-permute-start.4 = (bf16[1,128,256]{2,1,0:T(8,128)(2,1)S(1)}, bf16[1,128,256]{2,1,0:T(8,128)(2,1)S(1)}, u32[]{:S(2)}, u32[]{:S(2)}) collective-permute-start(bf16[1,128,256]{2,1,0:T(8,128)(2,1)S(1)} %get-tuple-element.31), channel_id=1, source_target_pairs={{0,20},{4,16},{8,28},{12,24},{16,4},{20,0},{24,12},{28,8},{1,21},{... | collective-permute-start | bytes 196616 | tf_op jit(solution)/shard_map/ppermute | solution.py:59
  43.3 9.0 %collective-permute-start.5 = (bf16[1,128,256]{2,1,0:T(8,128)(2,1)S(1)}, bf16[1,128,256]{2,1,0:T(8,128)(2,1)S(1)}, u32[]{:S(2)}, u32[]{:S(2)}) collective-permute-start(bf16[1,128,256]{2,1,0:T(8,128)(2,1)S(1)} %get-tuple-element.30), channel_id=1, source_target_pairs={{0,24},{4,28},{8,16},{12,20},{16,8},{20,12},{24,0},{28,4},{1,25},{... | collective-permute-start | bytes 196616 | tf_op jit(solution)/shard_map/ppermute | solution.py:59
  46.6 7.1 %collective-permute-start.6 = (bf16[1,128,256]{2,1,0:T(8,128)(2,1)S(1)}, bf16[1,128,256]{2,1,0:T(8,128)(2,1)S(1)}, u32[]{:S(2)}, u32[]{:S(2)}) collective-permute-start(bf16[1,128,256]{2,1,0:T(8,128)(2,1)S(1)} %get-tuple-element.29), channel_id=1, source_target_pairs={{0,28},{4,24},{8,20},{12,16},{16,12},{20,8},{24,4},{28,0},{1,29},{... | collective-permute-start | bytes 196616 | tf_op jit(solution)/shard_map/ppermute | solution.py:59
  62.4 3.3 %copy-start.1 = (f32[768,256]{1,0:T(8,128)S(1)}, f32[768,256]{1,0:T(8,128)}, u32[]{:S(2)}) copy-start(f32[768,256]{1,0:T(8,128)} %param.7) | copy-start | bytes 2359300
  62.4 3.3 %copy-start.6 = (s32[768]{0:T(1024)S(1)}, s32[768]{0:T(1024)}, u32[]{:S(2)}) copy-start(s32[768]{0:T(1024)} %param.8) | copy-start | bytes 9220
  67.5 73.0 %all-gather.9.cloned.1.call-start = ((), (), s32[]{:S(2)}) async-start(), calls=%async_computation.3 | async-start | bytes 1966080 | tf_op jit(solution)/shard_map/all_gather | solution.py:47
  89.0 19.2 %copy-start.4 = (bf16[24,128,256]{2,1,0:T(8,128)(2,1)S(1)}, bf16[24,128,256]{2,1,0:T(8,128)(2,1)}, u32[]{:S(2)}) copy-start(bf16[24,128,256]{2,1,0:T(8,128)(2,1)} %all-gather.7.cloned.1.call-done) | copy-start | bytes 4718596
  90.2 7.4 %collective-permute-start.7 = (bf16[1,128,256]{2,1,0:T(8,128)(2,1)S(1)}, bf16[1,128,256]{2,1,0:T(8,128)(2,1)S(1)}, u32[]{:S(2)}, u32[]{:S(2)}) collective-permute-start(bf16[1,128,256]{2,1,0:T(8,128)(2,1)S(1)} %get-tuple-element.27), channel_id=1, source_target_pairs={{0,4},{4,0},{8,12},{12,8},{16,20},{20,16},{24,28},{28,24},{1,5},{5... | collective-permute-start | bytes 196616 | tf_op jit(solution)/shard_map/ppermute | solution.py:59
  91.8 9.2 %collective-permute-start.8 = (bf16[1,128,256]{2,1,0:T(8,128)(2,1)S(1)}, bf16[1,128,256]{2,1,0:T(8,128)(2,1)S(1)}, u32[]{:S(2)}, u32[]{:S(2)}) collective-permute-start(bf16[1,128,256]{2,1,0:T(8,128)(2,1)S(1)} %get-tuple-element.26), channel_id=1, source_target_pairs={{0,8},{4,12},{8,0},{12,4},{16,24},{20,28},{24,16},{28,20},{1,9},{5... | collective-permute-start | bytes 196616 | tf_op jit(solution)/shard_map/ppermute | solution.py:59
  93.3 8.3 %collective-permute-start.9 = (bf16[1,128,256]{2,1,0:T(8,128)(2,1)S(1)}, bf16[1,128,256]{2,1,0:T(8,128)(2,1)S(1)}, u32[]{:S(2)}, u32[]{:S(2)}) collective-permute-start(bf16[1,128,256]{2,1,0:T(8,128)(2,1)S(1)} %get-tuple-element.25), channel_id=1, source_target_pairs={{0,12},{4,8},{8,4},{12,0},{16,28},{20,24},{24,20},{28,16},{1,13},{... | collective-permute-start | bytes 196616 | tf_op jit(solution)/shard_map/ppermute | solution.py:59
  93.8 7.8 %collective-permute-start.10 = (bf16[1,128,256]{2,1,0:T(8,128)(2,1)S(1)}, bf16[1,128,256]{2,1,0:T(8,128)(2,1)S(1)}, u32[]{:S(2)}, u32[]{:S(2)}) collective-permute-start(bf16[1,128,256]{2,1,0:T(8,128)(2,1)S(1)} %get-tuple-element.24), channel_id=1, source_target_pairs={{0,16},{4,20},{8,24},{12,28},{16,0},{20,4},{24,8},{28,12},{1,17},{... | collective-permute-start | bytes 196616 | tf_op jit(solution)/shard_map/ppermute | solution.py:59
  96.2 10.4 %collective-permute-start.11 = (bf16[1,128,256]{2,1,0:T(8,128)(2,1)S(1)}, bf16[1,128,256]{2,1,0:T(8,128)(2,1)S(1)}, u32[]{:S(2)}, u32[]{:S(2)}) collective-permute-start(bf16[1,128,256]{2,1,0:T(8,128)(2,1)S(1)} %get-tuple-element.23), channel_id=1, source_target_pairs={{0,20},{4,16},{8,28},{12,24},{16,4},{20,0},{24,12},{28,8},{1,21},{... | collective-permute-start | bytes 196616 | tf_op jit(solution)/shard_map/ppermute | solution.py:59
  97.6 9.0 %collective-permute-start.12 = (bf16[1,128,256]{2,1,0:T(8,128)(2,1)S(1)}, bf16[1,128,256]{2,1,0:T(8,128)(2,1)S(1)}, u32[]{:S(2)}, u32[]{:S(2)}) collective-permute-start(bf16[1,128,256]{2,1,0:T(8,128)(2,1)S(1)} %get-tuple-element.22), channel_id=1, source_target_pairs={{0,24},{4,28},{8,16},{12,20},{16,8},{20,12},{24,0},{28,4},{1,25},{... | collective-permute-start | bytes 196616 | tf_op jit(solution)/shard_map/ppermute | solution.py:59
  101.0 7.1 %collective-permute-start.13 = (bf16[1,128,256]{2,1,0:T(8,128)(2,1)S(1)}, bf16[1,128,256]{2,1,0:T(8,128)(2,1)S(1)}, u32[]{:S(2)}, u32[]{:S(2)}) collective-permute-start(bf16[1,128,256]{2,1,0:T(8,128)(2,1)S(1)} %get-tuple-element.21), channel_id=1, source_target_pairs={{0,28},{4,24},{8,20},{12,16},{16,12},{20,8},{24,4},{28,0},{1,29},{... | collective-permute-start | bytes 196616 | tf_op jit(solution)/shard_map/ppermute | solution.py:59
  121.8 72.9 %all-gather.11.cloned.1.call-start = ((), (), s32[]{:S(2)}) async-start(), calls=%async_computation.4 | async-start | bytes 1966080 | tf_op jit(solution)/shard_map/all_gather | solution.py:47
  143.3 19.2 %copy-start.5 = (bf16[24,128,256]{2,1,0:T(8,128)(2,1)S(1)}, bf16[24,128,256]{2,1,0:T(8,128)(2,1)}, u32[]{:S(2)}) copy-start(bf16[24,128,256]{2,1,0:T(8,128)(2,1)} %all-gather.9.cloned.1.call-done) | copy-start | bytes 4718596
  144.5 7.4 %collective-permute-start.14 = (bf16[1,128,256]{2,1,0:T(8,128)(2,1)S(1)}, bf16[1,128,256]{2,1,0:T(8,128)(2,1)S(1)}, u32[]{:S(2)}, u32[]{:S(2)}) collective-permute-start(bf16[1,128,256]{2,1,0:T(8,128)(2,1)S(1)} %get-tuple-element.19), channel_id=1, source_target_pairs={{0,4},{4,0},{8,12},{12,8},{16,20},{20,16},{24,28},{28,24},{1,5},{5... | collective-permute-start | bytes 196616 | tf_op jit(solution)/shard_map/ppermute | solution.py:59
  146.1 9.2 %collective-permute-start.15 = (bf16[1,128,256]{2,1,0:T(8,128)(2,1)S(1)}, bf16[1,128,256]{2,1,0:T(8,128)(2,1)S(1)}, u32[]{:S(2)}, u32[]{:S(2)}) collective-permute-start(bf16[1,128,256]{2,1,0:T(8,128)(2,1)S(1)} %get-tuple-element.18), channel_id=1, source_target_pairs={{0,8},{4,12},{8,0},{12,4},{16,24},{20,28},{24,16},{28,20},{1,9},{5... | collective-permute-start | bytes 196616 | tf_op jit(solution)/shard_map/ppermute | solution.py:59
  147.6 8.3 %collective-permute-start.16 = (bf16[1,128,256]{2,1,0:T(8,128)(2,1)S(1)}, bf16[1,128,256]{2,1,0:T(8,128)(2,1)S(1)}, u32[]{:S(2)}, u32[]{:S(2)}) collective-permute-start(bf16[1,128,256]{2,1,0:T(8,128)(2,1)S(1)} %get-tuple-element.17), channel_id=1, source_target_pairs={{0,12},{4,8},{8,4},{12,0},{16,28},{20,24},{24,20},{28,16},{1,13},{... | collective-permute-start | bytes 196616 | tf_op jit(solution)/shard_map/ppermute | solution.py:59
  148.1 7.8 %collective-permute-start.17 = (bf16[1,128,256]{2,1,0:T(8,128)(2,1)S(1)}, bf16[1,128,256]{2,1,0:T(8,128)(2,1)S(1)}, u32[]{:S(2)}, u32[]{:S(2)}) collective-permute-start(bf16[1,128,256]{2,1,0:T(8,128)(2,1)S(1)} %get-tuple-element.16), channel_id=1, source_target_pairs={{0,16},{4,20},{8,24},{12,28},{16,0},{20,4},{24,8},{28,12},{1,17},{... | collective-permute-start | bytes 196616 | tf_op jit(solution)/shard_map/ppermute | solution.py:59
  150.5 10.4 %collective-permute-start.18 = (bf16[1,128,256]{2,1,0:T(8,128)(2,1)S(1)}, bf16[1,128,256]{2,1,0:T(8,128)(2,1)S(1)}, u32[]{:S(2)}, u32[]{:S(2)}) collective-permute-start(bf16[1,128,256]{2,1,0:T(8,128)(2,1)S(1)} %get-tuple-element.15), channel_id=1, source_target_pairs={{0,20},{4,16},{8,28},{12,24},{16,4},{20,0},{24,12},{28,8},{1,21},{... | collective-permute-start | bytes 196616 | tf_op jit(solution)/shard_map/ppermute | solution.py:59
  151.9 9.0 %collective-permute-start.19 = (bf16[1,128,256]{2,1,0:T(8,128)(2,1)S(1)}, bf16[1,128,256]{2,1,0:T(8,128)(2,1)S(1)}, u32[]{:S(2)}, u32[]{:S(2)}) collective-permute-start(bf16[1,128,256]{2,1,0:T(8,128)(2,1)S(1)} %get-tuple-element.14), channel_id=1, source_target_pairs={{0,24},{4,28},{8,16},{12,20},{16,8},{20,12},{24,0},{28,4},{1,25},{... | collective-permute-start | bytes 196616 | tf_op jit(solution)/shard_map/ppermute | solution.py:59
  155.3 7.1 %collective-permute-start.20 = (bf16[1,128,256]{2,1,0:T(8,128)(2,1)S(1)}, bf16[1,128,256]{2,1,0:T(8,128)(2,1)S(1)}, u32[]{:S(2)}, u32[]{:S(2)}) collective-permute-start(bf16[1,128,256]{2,1,0:T(8,128)(2,1)S(1)} %get-tuple-element.13), channel_id=1, source_target_pairs={{0,28},{4,24},{8,20},{12,16},{16,12},{20,8},{24,4},{28,0},{1,29},{... | collective-permute-start | bytes 196616 | tf_op jit(solution)/shard_map/ppermute | solution.py:59
  197.6 19.2 %copy-start.3 = (bf16[24,128,256]{2,1,0:T(8,128)(2,1)S(1)}, bf16[24,128,256]{2,1,0:T(8,128)(2,1)}, u32[]{:S(2)}) copy-start(bf16[24,128,256]{2,1,0:T(8,128)(2,1)} %all-gather.11.cloned.1.call-done) | copy-start | bytes 4718596
  198.8 7.4 %collective-permute-start.21 = (bf16[1,128,256]{2,1,0:T(8,128)(2,1)S(1)}, bf16[1,128,256]{2,1,0:T(8,128)(2,1)S(1)}, u32[]{:S(2)}, u32[]{:S(2)}) collective-permute-start(bf16[1,128,256]{2,1,0:T(8,128)(2,1)S(1)} %get-tuple-element.11), channel_id=1, source_target_pairs={{0,4},{4,0},{8,12},{12,8},{16,20},{20,16},{24,28},{28,24},{1,5},{5... | collective-permute-start | bytes 196616 | tf_op jit(solution)/shard_map/ppermute | solution.py:59
  200.4 9.2 %collective-permute-start.22 = (bf16[1,128,256]{2,1,0:T(8,128)(2,1)S(1)}, bf16[1,128,256]{2,1,0:T(8,128)(2,1)S(1)}, u32[]{:S(2)}, u32[]{:S(2)}) collective-permute-start(bf16[1,128,256]{2,1,0:T(8,128)(2,1)S(1)} %get-tuple-element.10), channel_id=1, source_target_pairs={{0,8},{4,12},{8,0},{12,4},{16,24},{20,28},{24,16},{28,20},{1,9},{5... | collective-permute-start | bytes 196616 | tf_op jit(solution)/shard_map/ppermute | solution.py:59
  201.8 8.3 %collective-permute-start.23 = (bf16[1,128,256]{2,1,0:T(8,128)(2,1)S(1)}, bf16[1,128,256]{2,1,0:T(8,128)(2,1)S(1)}, u32[]{:S(2)}, u32[]{:S(2)}) collective-permute-start(bf16[1,128,256]{2,1,0:T(8,128)(2,1)S(1)} %get-tuple-element.9), channel_id=1, source_target_pairs={{0,12},{4,8},{8,4},{12,0},{16,28},{20,24},{24,20},{28,16},{1,13},{... | collective-permute-start | bytes 196616 | tf_op jit(solution)/shard_map/ppermute | solution.py:59
  202.4 7.8 %collective-permute-start.24 = (bf16[1,128,256]{2,1,0:T(8,128)(2,1)S(1)}, bf16[1,128,256]{2,1,0:T(8,128)(2,1)S(1)}, u32[]{:S(2)}, u32[]{:S(2)}) collective-permute-start(bf16[1,128,256]{2,1,0:T(8,128)(2,1)S(1)} %get-tuple-element.8), channel_id=1, source_target_pairs={{0,16},{4,20},{8,24},{12,28},{16,0},{20,4},{24,8},{28,12},{1,17},{... | collective-permute-start | bytes 196616 | tf_op jit(solution)/shard_map/ppermute | solution.py:59
  204.8 10.4 %collective-permute-start.25 = (bf16[1,128,256]{2,1,0:T(8,128)(2,1)S(1)}, bf16[1,128,256]{2,1,0:T(8,128)(2,1)S(1)}, u32[]{:S(2)}, u32[]{:S(2)}) collective-permute-start(bf16[1,128,256]{2,1,0:T(8,128)(2,1)S(1)} %get-tuple-element.7), channel_id=1, source_target_pairs={{0,20},{4,16},{8,28},{12,24},{16,4},{20,0},{24,12},{28,8},{1,21},{... | collective-permute-start | bytes 196616 | tf_op jit(solution)/shard_map/ppermute | solution.py:59
  206.2 9.0 %collective-permute-start.26 = (bf16[1,128,256]{2,1,0:T(8,128)(2,1)S(1)}, bf16[1,128,256]{2,1,0:T(8,128)(2,1)S(1)}, u32[]{:S(2)}, u32[]{:S(2)}) collective-permute-start(bf16[1,128,256]{2,1,0:T(8,128)(2,1)S(1)} %get-tuple-element.6), channel_id=1, source_target_pairs={{0,24},{4,28},{8,16},{12,20},{16,8},{20,12},{24,0},{28,4},{1,25},{... | collective-permute-start | bytes 196616 | tf_op jit(solution)/shard_map/ppermute | solution.py:59
  209.6 7.1 %collective-permute-start.27 = (bf16[1,128,256]{2,1,0:T(8,128)(2,1)S(1)}, bf16[1,128,256]{2,1,0:T(8,128)(2,1)S(1)}, u32[]{:S(2)}, u32[]{:S(2)}) collective-permute-start(bf16[1,128,256]{2,1,0:T(8,128)(2,1)S(1)} %get-tuple-element.5), channel_id=1, source_target_pairs={{0,28},{4,24},{8,20},{12,16},{16,12},{20,8},{24,4},{28,0},{1,29},{... | collective-permute-start | bytes 196616 | tf_op jit(solution)/shard_map/ppermute | solution.py:59
Sparse Core Ops, SparseCore 0:
  11.3 22.3 all-gather.4
  67.7 18.4 all-gather.6
  121.9 18.4 all-gather.8
  176.2 18.4 all-gather.10
